TPU v7x, 8 devices: a whole 2x2x1 slice. The times are simulated.
8 devices in a mesh: dp: 1 (over z), tp: 2 (over y), pp: 4 (over x, core).
Axes of the slice: x: 2, y: 2, z: 1, core: 2. Of those that a mesh axis runs over, the one named last changes fastest.
Arguments:
- hidden: bfloat16 [2, 128, 2048], P('dp')
- positions: int32 [2, 128], P('dp')
- key_cache: bfloat16 [4, 2, 128, 32, 32, 64], P('pp', 'dp', None, 'tp')
- value_cache: bfloat16 [4, 2, 128, 32, 32, 64], P('pp', 'dp', None, 'tp')
- attn_norm: bfloat16 [4, 2048], P('pp')
- w_query: bfloat16 [4, 2048, 2048], P('pp', None, 'tp')
- w_key: bfloat16 [4, 2048, 2048], P('pp', None, 'tp')
- w_value: bfloat16 [4, 2048, 2048], P('pp', None, 'tp')
- w_out: bfloat16 [4, 2048, 2048], P('pp', 'tp')
- mlp_norm: bfloat16 [4, 2048], P('pp')
- w_gate: bfloat16 [4, 2048, 8192], P('pp', None, 'tp')
- w_up: bfloat16 [4, 2048, 8192], P('pp', None, 'tp')
- w_down: bfloat16 [4, 8192, 2048], P('pp', 'tp')
Outputs:
- output 1: bfloat16 [2, 128, 2048], P('dp')
- output 2: bfloat16 [4, 2, 128, 32, 32, 64], P('pp', 'dp', None, 'tp')
- output 3: bfloat16 [4, 2, 128, 32, 32, 64], P('pp', 'dp', None, 'tp')
All inputs are finite; a program needn't handle non-finite values.
Results may differ from a plain program's by a relative error of at most 0.02.
Values are sent between devices in bfloat16 or wider.
A program may use at most 1 GiB of HBM per device.

v0:
```python
import functools
import math
import jax
import jax.numpy as jnp
import numpy as np
from jax import lax
from jax.experimental import pallas as pl
from jax.experimental.pallas import tpu as pltpu
from jax.sharding import PartitionSpec as P

ROPE_THETA = 500000.0
SCALE_FACTOR = 8.0
LOW_FACTOR = 1.0
HIGH_FACTOR = 4.0
ORIG_CONTEXT = 8192.0
NORM_EPS = 1e-5
MESH = pl.DeviceIdType.MESH
F32 = jnp.float32
BF16 = jnp.bfloat16

COLS = 512
SLOTS = 8
NORM_ROWS = 64
KEEP_SLOTS = 16
WRITE_SLOTS = 48


def rope_freqs(head_dim):
    freq_index = np.arange(head_dim // 2, dtype=np.float64)
    base_freq = ROPE_THETA ** (-2.0 * freq_index / head_dim)
    wave_len = 2.0 * math.pi / base_freq
    smooth_t = (ORIG_CONTEXT / wave_len - LOW_FACTOR) / (HIGH_FACTOR - LOW_FACTOR)
    mixed_freq = (1.0 - smooth_t) * base_freq / SCALE_FACTOR + smooth_t * base_freq
    long_freq = np.where(wave_len > ORIG_CONTEXT / LOW_FACTOR, base_freq / SCALE_FACTOR, mixed_freq)
    return np.where(wave_len < ORIG_CONTEXT / HIGH_FACTOR, base_freq, long_freq).astype(np.float32)


def layer_kernel(dims, after, pos_ref, ga_ref, gm_ref, hid, kc, vc, wq, wk, wv, wo, wg, wu, wd,
                 hout, knew, vnew,
                 wmix, wg_v, wu_v, ring, hbuf, recvp, recvd, nbuf, qt, ubuf, sc, cos_ref, sin_ref,
                 hid_sem, wqkv_sem, wo_sem, wd_sem, gu_sem, ring_sem,
                 p_send, p_recv, d_send, d_recv, h_send, h_recv):
    n_groups, n_batch, d_model, heads, seq, hd, ff, n_pp, n_tp = dims
    hw = heads * hd
    n_chunk = d_model // COLS
    n_gu = ff // COLS
    n_half = d_model // hw
    n_deep = ff // d_model
    pp = lax.axis_index("pp")
    tp = lax.axis_index("tp")
    peer = {"tp": lax.rem(tp + 1, n_tp)}
    nxt = {"pp": lax.rem(pp + 1, n_pp)}
    prv = {"pp": lax.rem(pp + n_pp - 1, n_pp)}

    n_kv = n_groups * heads

    def kv_copies(item, slot):
        g = item // heads
        h = lax.rem(item, heads)
        return (pltpu.make_async_copy(kc.at[g, h], ring.at[slot, pl.ds(0, seq)], ring_sem.at[slot, 0]),
                pltpu.make_async_copy(vc.at[g, h], ring.at[slot, pl.ds(seq, seq)], ring_sem.at[slot, 1]))

    def wd_copy(i):
        return pltpu.make_async_copy(wd.at[pl.ds(i % n_deep * d_model, d_model), pl.ds(i // n_deep * hw, hw)], wmix.at[i], wd_sem.at[i])

    def gu_copies(j):
        cols = pl.ds(pl.multiple_of(j * COLS, COLS), COLS)
        return (pltpu.make_async_copy(wg.at[:, cols], wg_v.at[j], gu_sem.at[0, j]),
                pltpu.make_async_copy(wu.at[:, cols], wu_v.at[j], gu_sem.at[1, j]))

    def qkv_copies():
        return [pltpu.make_async_copy(src, wmix.at[i], wqkv_sem.at[i]) for i, src in enumerate((wq, wk, wv))]

    def wo_copies():
        return [pltpu.make_async_copy(wo.at[:, pl.ds(i * hw, hw)], wmix.at[3, pl.ds(i * hw, hw)], wo_sem.at[i]) for i in range(n_half)]

    def hid_copy(g):
        return pltpu.make_async_copy(hid.at[g], hbuf.at[g], hid_sem.at[g])

    def piece(ref, g, c):
        return ref.at[g, :, pl.ds(pl.multiple_of(c * COLS, COLS), COLS)]

    def p_copy(g, c):
        return pltpu.make_async_remote_copy(piece(hout, g, c), piece(recvp, g, c), p_send.at[g, c], p_recv.at[g, c], device_id=peer, device_id_type=MESH)

    def d_copy(g, c):
        return pltpu.make_async_remote_copy(piece(recvp, g, c), piece(recvd, g, c), d_send.at[g, c], d_recv.at[g, c], device_id=peer, device_id_type=MESH)

    def h_copy(g, c):
        return pltpu.make_async_remote_copy(piece(hout, g, c), piece(hbuf, g, c), h_send.at[g, c], h_recv.at[g, c], device_id=nxt, device_id_type=MESH)

    first = pp == 0
    last = pp == n_pp - 1

    @pl.when(first)
    def _():
        for g in range(n_groups):
            hid_copy(g).start()
    for copy in qkv_copies():
        copy.start()

    def start_kv_wo():
        for slot in range(SLOTS):
            for copy in kv_copies(slot, slot):
                copy.start()
        for copy in wo_copies():
            copy.start()

    @pl.when(pp > 0)
    def _():
        start_kv_wo()
        for j in range(n_gu):
            for copy in gu_copies(j):
                copy.start()

    freq_id = lax.broadcasted_iota(jnp.int32, (hd // 2, n_batch), 0)
    freqs = jnp.zeros((hd // 2, n_batch), F32)
    for i, freq in enumerate(rope_freqs(hd)):
        freqs = jnp.where(freq_id == i, float(freq), freqs)
    for g in range(n_groups):
        angles = pos_ref[g].astype(F32) * freqs
        cos_ref[g] = jnp.cos(angles)
        sin_ref[g] = jnp.sin(angles)

    barrier = pltpu.get_barrier_semaphore()
    pl.semaphore_signal(barrier, inc=1, device_id=peer, device_id_type=MESH)

    @pl.when(jnp.logical_not(last))
    def _():
        pl.semaphore_signal(barrier, inc=1, device_id=nxt, device_id_type=MESH)

    @pl.when(pp > 0)
    def _():
        pl.semaphore_signal(barrier, inc=1, device_id=prv, device_id_type=MESH)
    ends = jnp.logical_or(first, last)

    @pl.when(ends)
    def _():
        pl.semaphore_wait(barrier, 2)

    @pl.when(jnp.logical_not(ends))
    def _():
        pl.semaphore_wait(barrier, 3)

    def norm_rows(g, gain_ref, with_partial):
        def body(r, carry):
            rows = pl.ds(pl.multiple_of(r * NORM_ROWS, NORM_ROWS), NORM_ROWS)
            x = hbuf[g, rows, :].astype(F32)
            if with_partial:
                part = (hout[g, rows, :].astype(F32) + recvp[g, rows, :].astype(F32)).astype(BF16)
                x = (x + part.astype(F32)).astype(BF16)
                hbuf[g, rows, :] = x
                x = x.astype(F32)
            inv = lax.rsqrt(jnp.mean(x * x, axis=-1, keepdims=True) + NORM_EPS)
            nbuf[rows, :] = (x * inv * gain_ref[...].astype(F32)).astype(BF16)
            return carry
        lax.fori_loop(0, n_batch // NORM_ROWS, body, 0)

    def attention_phase(g, carry):
        @pl.when(first)
        def _():
            hid_copy(g).wait()

        @pl.when(pp > 0)
        def _():
            for c in range(n_chunk):
                h_copy(g, c).wait_recv()

        norm_rows(g, ga_ref, False)
        cosine = cos_ref[g]
        sine = sin_ref[g]
        half = hd // 2

        @pl.when(g == 0)
        def _():
            for i, copy in enumerate(qkv_copies()):
                copy.wait()
                if i == 0:
                    pl.when(first)(start_kv_wo)

        for which in range(3):
            for c in range(hw // COLS):
                cols = slice(c * COLS, (c + 1) * COLS)
                prod_t = jnp.dot(nbuf[...], wmix[which, :, cols], preferred_element_type=F32).T
                for i in range(COLS // hd):
                    head = c * (COLS // hd) + i
                    a = prod_t[i * hd:i * hd + half]
                    b = prod_t[i * hd + half:(i + 1) * hd]
                    if which < 2:
                        a, b = a * cosine - b * sine, b * cosine + a * sine
                    both = jnp.concatenate([a, b], axis=0).astype(BF16)
                    if which == 0:
                        qt[head * hd:(head + 1) * hd, :] = both
                    else:
                        dst = knew if which == 1 else vnew
                        dst[g, head] = both

        pos = pos_ref[g]
        row_id = lax.broadcasted_iota(jnp.int32, (seq, n_batch), 0)
        hit = row_id == pos
        seen = row_id <= pos

        def head_body(h, inner):
            item = g * heads + h
            slot = lax.rem(item, SLOTS)
            for copy in kv_copies(item, slot):
                copy.wait()
            rows = pl.ds(pl.multiple_of(h * hd, hd), hd)
            q = qt[rows, :].astype(F32)
            fresh = jnp.sum(q * knew[g, h].astype(F32), axis=0, keepdims=True)
            for s in range(seq):
                total = None
                for d in range(4):
                    piece_d = ring[slot, s, d * 16:(d + 1) * 16].astype(F32) * q[d * 16:(d + 1) * 16]
                    total = piece_d if total is None else total + piece_d
                sc[s:s + 1, :] = jnp.sum(total, axis=0, keepdims=True)
            scores = jnp.where(hit, fresh, sc[...]) * hd ** -0.5
            scores = jnp.where(seen, scores, -jnp.inf)
            top = jnp.max(scores, axis=0, keepdims=True)
            expd = jnp.exp(scores - top)
            probs = (expd / jnp.sum(expd, axis=0, keepdims=True)).astype(BF16).astype(F32)
            sc[...] = jnp.where(hit, 0.0, probs)
            acc = jnp.sum(jnp.where(hit, probs, 0.0), axis=0, keepdims=True) * vnew[g, h].astype(F32)
            quarter = hd // 4
            for d in range(4):
                some = acc[d * quarter:(d + 1) * quarter]
                for s in range(seq):
                    some = some + sc[s:s + 1, :] * ring[slot, seq + s, d * quarter:(d + 1) * quarter].astype(F32)
                qt[pl.ds(pl.multiple_of(h * hd + d * quarter, quarter), quarter), :] = some.astype(BF16)

            @pl.when(item + SLOTS < n_kv)
            def _():
                for copy in kv_copies(item + SLOTS, slot):
                    copy.start()

            @pl.when(jnp.logical_and(jnp.logical_and(first, item + SLOTS < n_kv), lax.rem(item, SLOTS) == SLOTS // 2))
            def _():
                for copy in gu_copies(item // SLOTS):
                    copy.start()

            @pl.when(item + SLOTS == n_kv)
            def _():
                @pl.when(first)
                def _():
                    for j in range((n_kv - SLOTS) // SLOTS, n_gu):
                        for copy in gu_copies(j):
                            copy.start()
                for i in range(3):
                    wd_copy(i).start()
            return inner
        lax.fori_loop(0, heads, head_body, 0)

        @pl.when(g == 0)
        def _():
            for copy in wo_copies():
                copy.wait()
        for c in range(hw // COLS):
            cols = slice(c * COLS, (c + 1) * COLS)
            nbuf[:, cols] = qt[cols, :].astype(F32).T.astype(BF16)

        for c in range(n_chunk):
            at, col = divmod(c * COLS, hw)
            part = jnp.dot(nbuf[:, 0:hw], wmix[3, at * hw:(at + 1) * hw, col:col + COLS], preferred_element_type=F32)
            hout[g, :, c * COLS:(c + 1) * COLS] = part.astype(BF16)
        for c in range(n_chunk):
            p_copy(g, c).start()

        @pl.when(g == n_groups - 1)
        def _():
            wd_copy(3).start()
        return carry

    def mlp_phase(g, carry):
        for c in range(n_chunk):
            p_copy(g, c).wait()
        norm_rows(g, gm_ref, True)

        some = n_gu // 2

        def finish_some(part):
            @pl.when(g > 0)
            def _():
                for c in range(n_chunk // 2):
                    finish_piece(g - 1, part * (n_chunk // 2) + c)

        def gu_body(part, inner):
            tiles = [part * some + i for i in range(some)]

            @pl.when(g == 0)
            def _():
                for j in tiles:
                    for copy in gu_copies(j):
                        copy.wait()
            pl.when(part > 0)(lambda: finish_some(part - 1))
            for j in tiles:
                gate = jnp.dot(nbuf[...], wg_v[j], preferred_element_type=F32)
                up = jnp.dot(nbuf[...], wu_v[j], preferred_element_type=F32)
                ubuf[:, pl.ds(pl.multiple_of(j * COLS, COLS), COLS)] = (jax.nn.silu(gate) * up).astype(BF16)
            return inner
        lax.fori_loop(0, 2, gu_body, 0)
        finish_some(1)

        for c in range(n_chunk):
            at, col = divmod(c * COLS, hw)
            if col == 0:
                @pl.when(g == 0)
                def _():
                    for i in range(n_deep):
                        wd_copy(at * n_deep + i).wait()
            acc = None
            for i in range(n_deep):
                prod = jnp.dot(ubuf[:, i * d_model:(i + 1) * d_model], wmix[at * n_deep + i, :, col:col + COLS], preferred_element_type=F32)
                acc = prod if acc is None else acc + prod
            recvp[g, :, c * COLS:(c + 1) * COLS] = acc.astype(BF16)
            d_copy(g, c).start()
        return carry

    def finish_piece(g, c):
        d_copy(g, c).wait()
        cols = pl.ds(pl.multiple_of(c * COLS, COLS), COLS)
        part = (recvd[g, :, cols].astype(F32) + recvp[g, :, cols].astype(F32)).astype(BF16)
        hout[g, :, cols] = (hbuf[g, :, cols].astype(F32) + part.astype(F32)).astype(BF16)

        @pl.when(jnp.logical_not(last))
        def _():
            h_copy(g, c).start()

    lax.fori_loop(0, n_groups, attention_phase, 0)
    lax.fori_loop(0, n_groups, mlp_phase, 0)
    for c in range(n_chunk):
        finish_piece(n_groups - 1, c)

    @pl.when(jnp.logical_not(last))
    def _():
        for g in range(n_groups):
            for c in range(n_chunk):
                h_copy(g, c).wait_send()


def run_layer(dims, *args):
    n_groups, n_batch, d_model, heads, seq, hd, ff, n_pp, n_tp = dims
    hw = heads * hd
    n_chunk = d_model // COLS
    n_gu = ff // COLS
    assert ff * d_model == 4 * d_model * hw
    vmem = pl.BlockSpec(memory_space=pltpu.VMEM)
    hbm = pl.BlockSpec(memory_space=pltpu.HBM)
    dma = pltpu.SemaphoreType.DMA
    return pl.pallas_call(
        functools.partial(layer_kernel, dims),
        out_shape=(jax.ShapeDtypeStruct((n_groups, n_batch, d_model), BF16),
                   jax.ShapeDtypeStruct((n_groups, heads, hd, n_batch), BF16),
                   jax.ShapeDtypeStruct((n_groups, heads, hd, n_batch), BF16)),
        in_specs=[hbm] + [vmem] * 3 + [hbm] * 10,
        out_specs=(vmem, vmem, vmem),
        scratch_shapes=[
            pltpu.VMEM((4, d_model, hw), BF16),
            pltpu.VMEM((n_gu, d_model, COLS), BF16),
            pltpu.VMEM((n_gu, d_model, COLS), BF16),
            pltpu.VMEM((SLOTS, 2 * seq, hd, n_batch), BF16),
            pltpu.VMEM((n_groups, n_batch, d_model), BF16),
            pltpu.VMEM((n_groups, n_batch, d_model), BF16),
            pltpu.VMEM((n_groups, n_batch, d_model), BF16),
            pltpu.VMEM((n_batch, d_model), BF16),
            pltpu.VMEM((hw, n_batch), BF16),
            pltpu.VMEM((n_batch, ff), BF16),
            pltpu.VMEM((seq, n_batch), F32),
            pltpu.VMEM((n_groups, hd // 2, n_batch), F32),
            pltpu.VMEM((n_groups, hd // 2, n_batch), F32),
            dma((n_groups,)), dma((3,)), dma((d_model // hw,)), dma((4,)), dma((2, n_gu)), dma((SLOTS, 2)),
            dma((n_groups, n_chunk)), dma((n_groups, n_chunk)), dma((n_groups, n_chunk)),
            dma((n_groups, n_chunk)), dma((n_groups, n_chunk)), dma((n_groups, n_chunk)),
        ],
        compiler_params=pltpu.CompilerParams(collective_id=0, has_side_effects=True, vmem_limit_bytes=67043328),
        name="layer",
    )(*args)


def keep_kernel(dims, pos_hbm, kc, vc, kout, vout, todo_hbm, kb, vb, pos, todo, flags, in_sem, out_sem, pos_sem, todo_sem):
    n_groups, n_batch, _, heads, seq, _, _, n_pp, _ = dims
    n_slab = n_groups * seq
    n_items = n_groups * heads
    ahead = KEEP_SLOTS // 2
    last = lax.axis_index("pp") == n_pp - 1

    def loads(i):
        slot = lax.rem(i, KEEP_SLOTS)
        g, h = i // heads, lax.rem(i, heads)
        return (pltpu.make_async_copy(kc.at[g, h], kb.at[slot], in_sem.at[0, slot]),
                pltpu.make_async_copy(vc.at[g, h], vb.at[slot], in_sem.at[1, slot]))

    def stores(i):
        slot = lax.rem(i, KEEP_SLOTS)
        g, h = i // heads, lax.rem(i, heads)
        return (pltpu.make_async_copy(kb.at[slot], kout.at[g, h], out_sem.at[0, slot]),
                pltpu.make_async_copy(vb.at[slot], vout.at[g, h], out_sem.at[1, slot]))

    @pl.when(last)
    def _():
        for i in range(ahead):
            for copy in loads(i):
                copy.start()

        pos_copy = pltpu.make_async_copy(pos_hbm, pos, pos_sem)
        pos_copy.start()
        pos_copy.wait()

        def clear(i, carry):
            flags[i] = 0
            todo[i + 1] = 0
            return carry
        lax.fori_loop(0, n_slab, clear, 0)
        for g in range(n_groups):
            def mark(b, carry):
                flags[g * seq + pos[g, b]] = 1
                return carry
            lax.fori_loop(0, n_batch, mark, 0)

        def pick(i, count):
            hit = flags[i]

            @pl.when(hit == 1)
            def _():
                todo[count + 1] = i
            return count + hit
        todo[0] = lax.fori_loop(0, n_slab, pick, jnp.int32(0))
        todo_copy = pltpu.make_async_copy(todo, todo_hbm, todo_sem)
        todo_copy.start()

        def body(i, carry):
            for copy in loads(i):
                copy.wait()
            for copy in stores(i):
                copy.start()

            @pl.when(i + ahead < n_items)
            def _():
                @pl.when(i >= ahead)
                def _():
                    for copy in stores(i - ahead):
                        copy.wait()
                for copy in loads(i + ahead):
                    copy.start()
            return carry
        lax.fori_loop(0, n_items, body, 0)
        for i in range(n_items - 2 * ahead, n_items):
            for copy in stores(i):
                copy.wait()
        todo_copy.wait()


def keep_old(dims, positions, key_t, value_t):
    n_groups, n_batch, _, heads, seq, hd, _, _, _ = dims
    hbm = pl.BlockSpec(memory_space=pltpu.HBM)
    dma = pltpu.SemaphoreType.DMA
    return pl.pallas_call(
        functools.partial(keep_kernel, dims),
        out_shape=(jax.ShapeDtypeStruct(key_t.shape, BF16), jax.ShapeDtypeStruct(value_t.shape, BF16),
                   jax.ShapeDtypeStruct((n_groups * seq + 1,), jnp.int32)),
        in_specs=[hbm] * 3,
        out_specs=(hbm, hbm, hbm),
        scratch_shapes=[
            pltpu.VMEM((KEEP_SLOTS, seq, hd, n_batch), BF16),
            pltpu.VMEM((KEEP_SLOTS, seq, hd, n_batch), BF16),
            pltpu.SMEM((n_groups, n_batch), jnp.int32),
            pltpu.SMEM((n_groups * seq + 1,), jnp.int32),
            pltpu.SMEM((n_groups * seq,), jnp.int32),
            dma((2, KEEP_SLOTS)), dma((2, KEEP_SLOTS)), dma, dma,
        ],
        compiler_params=pltpu.CompilerParams(vmem_limit_bytes=67043328),
        name="cache_keep",
    )(positions, key_t, value_t)


def write_kernel(dims, todo_hbm, pos_hbm, knew_hbm, vnew_hbm, kc, vc, kold, vold, kout, vout,
                 todo, pos_ref, knew, vnew, kb, vb, in_sem, out_sem, small_sem):
    n_groups, _, _, _, seq, _, _, n_pp, _ = dims
    ahead = WRITE_SLOTS // 2
    last = lax.axis_index("pp") == n_pp - 1
    small = [pltpu.make_async_copy(src, dst, small_sem.at[i]) for i, (src, dst) in enumerate(
        ((todo_hbm, todo), (pos_hbm, pos_ref), (knew_hbm, knew), (vnew_hbm, vnew)))]
    for copy in small:
        copy.start()
    small[0].wait()
    count = jnp.where(last, todo[0], n_groups * seq)

    def place(i):
        entry = jnp.where(last, todo[i + 1], i)
        return entry // seq, lax.rem(entry, seq), lax.rem(i, WRITE_SLOTS)

    def loads(i):
        g, s, slot = place(i)
        return (pltpu.make_async_copy(kc.at[g, :, s], kb.at[slot], in_sem.at[0, slot]),
                pltpu.make_async_copy(vc.at[g, :, s], vb.at[slot], in_sem.at[1, slot]))

    def stores(i):
        g, s, slot = place(i)
        return (pltpu.make_async_copy(kb.at[slot], kout.at[g, :, s], out_sem.at[0, slot]),
                pltpu.make_async_copy(vb.at[slot], vout.at[g, :, s], out_sem.at[1, slot]))

    for i in range(ahead):
        @pl.when(i < count)
        def _():
            for copy in loads(i):
                copy.start()

    for copy in small[1:]:
        copy.wait()

    def body(i, carry):
        g, s, slot = place(i)
        for copy in loads(i):
            copy.wait()
        hit = (pos_ref[g] == s)[None]
        for new, buf in ((knew, kb), (vnew, vb)):
            buf[slot] = jnp.where(hit, new[g].astype(F32), buf[slot].astype(F32)).astype(BF16)
        for copy in stores(i):
            copy.start()

        @pl.when(i + ahead < count)
        def _():
            @pl.when(i >= ahead)
            def _():
                for copy in stores(i - ahead):
                    copy.wait()
            for copy in loads(i + ahead):
                copy.start()
        return carry
    lax.fori_loop(0, count, body, 0)

    def drain(i, carry):
        for copy in stores(i):
            copy.wait()
        return carry
    lax.fori_loop(jnp.maximum(count - 2 * ahead, 0), count, drain, 0)


def write_new(dims, todo, pos, key_new, value_new, key_t, value_t, key_old, value_old):
    n_groups, n_batch, _, heads, seq, hd, _, _, _ = dims
    hbm = pl.BlockSpec(memory_space=pltpu.HBM)
    dma = pltpu.SemaphoreType.DMA
    return pl.pallas_call(
        functools.partial(write_kernel, dims),
        out_shape=(jax.ShapeDtypeStruct(key_t.shape, BF16), jax.ShapeDtypeStruct(value_t.shape, BF16)),
        in_specs=[hbm] * 8,
        out_specs=(hbm, hbm),
        scratch_shapes=[
            pltpu.SMEM((n_groups * seq + 1,), jnp.int32),
            pltpu.VMEM((n_groups, 1, n_batch), jnp.int32),
            pltpu.VMEM((n_groups, heads, hd, n_batch), BF16),
            pltpu.VMEM((n_groups, heads, hd, n_batch), BF16),
            pltpu.VMEM((WRITE_SLOTS, heads, hd, n_batch), BF16),
            pltpu.VMEM((WRITE_SLOTS, heads, hd, n_batch), BF16),
            dma((2, WRITE_SLOTS)), dma((2, WRITE_SLOTS)), dma((4,)),
        ],
        input_output_aliases={6: 0, 7: 1},
        compiler_params=pltpu.CompilerParams(vmem_limit_bytes=67043328),
        cost_estimate=pl.CostEstimate(flops=n_groups * n_batch * heads * seq * hd * 40, bytes_accessed=8 * key_t.size, transcendentals=0),
        name="cache_write",
    )(todo, pos, key_new, value_new, key_t, value_t, key_old, value_old)


def solution(mesh):
    n_pp = mesh.shape["pp"]
    n_tp = mesh.shape["tp"]
    cache_spec = P("pp", "dp", None, "tp", None, None)
    col_spec = P("pp", None, "tp")
    row_spec = P("pp", "tp", None)
    gain_spec = P("pp", None)
    in_specs = (P("dp", None, None), P("dp", None), cache_spec, cache_spec, gain_spec, col_spec, col_spec, col_spec, row_spec, gain_spec, col_spec, col_spec, row_spec)
    out_specs = (P("dp", None, None), cache_spec, cache_spec)

    def per_device(hidden, positions, key_cache, value_cache, attn_norm, w_query, w_key, w_value, w_out, mlp_norm, w_gate, w_up, w_down):
        _, n_groups, n_batch, heads, seq, hd = key_cache.shape
        d_model = hidden.shape[-1]
        ff = w_gate.shape[-1]
        dims = (n_groups, n_batch, d_model, heads, seq, hd, ff, n_pp, n_tp)
        key_t = jnp.transpose(key_cache[0], (0, 2, 3, 4, 1))
        value_t = jnp.transpose(value_cache[0], (0, 2, 3, 4, 1))
        pos = positions[:, None, :]
        key_old, value_old, todo = keep_old(dims, positions, key_t, value_t)
        state, key_new, value_new = run_layer(
            dims, todo, pos, attn_norm, mlp_norm, hidden, key_t, value_t,
            w_query[0], w_key[0], w_value[0], w_out[0], w_gate[0], w_up[0], w_down[0])

        stage = lax.axis_index("pp")
        from_last = [lax.ppermute(state, "pp", [(n_pp - 1, dst)]) for dst in range(1, n_pp - 1)]
        key_t, value_t = write_new(dims, todo, pos, key_new, value_new, key_t, value_t, key_old, value_old)
        from_last[0], key_t = lax.optimization_barrier((from_last[0], key_t))
        from_last.append(lax.ppermute(from_last[0], "pp", [(1, 0)]))
        final = jnp.where(stage == n_pp - 1, state, sum(from_last[1:], from_last[0]))
        return final, jnp.transpose(key_t, (0, 4, 1, 2, 3))[None], jnp.transpose(value_t, (0, 4, 1, 2, 3))[None]

    return jax.shard_map(per_device, mesh=mesh, in_specs=in_specs, out_specs=out_specs, check_vma=False)
```

profile of v0, /device:TPU:0, one launch (start us, length us, event | category | flops | bytes accessed | tf_op | source)
XLA Modules:
  0.0 171.7 jit_solution(6131983388660346447)
XLA Ops:
  0.6 0.6 cache_keep.1
  1.2 55.1 %layer.1 = (bf16[2,128,2048]{2,1,0:T(8,128)(2,1)}, bf16[2,16,64,128]{3,2,1,0:T(8,128)(2,1)}, bf16[2,16,64,128]{3,2,1,0:T(8,128)(2,1)}) custom-call(s32[65]{0:T(128)} %get-tuple-element.13.after.todo_hbm, s32[2,1,128]{2,1,0:T(1,128)} %bitcast.35, bf16[1,2048]{1,0:T(2,128)(2,1)} %ga_ref.1, bf16[1,2048]{1,0:T(2,128)(2,1)} %gm_ref.1, bf16[2,128,2048]{2,1,0:T(8,128)(2,1)} %hid.1, ...), custom_call_target="tpu_custom_call" | custom-call | tf_op jit(solution)/shard_map/layer/pallas_call | solution.py:349
  56.4 1.7 collective-permute-start
  58.1 1.6 collective-permute-start.1
  59.7 24.3 %cache_write.1 = (bf16[2,16,32,64,128]{4,3,2,1,0:T(8,128)(2,1)}, bf16[2,16,32,64,128]{4,3,2,1,0:T(8,128)(2,1)}) custom-call(s32[65]{0:T(128)} %get-tuple-element.13.after.todo_hbm, s32[2,1,128]{2,1,0:T(1,128)} %bitcast.36, bf16[2,16,64,128]{3,2,1,0:T(8,128)(2,1)} %get-tuple-element.15.knew_hbm, ...), custom_call_target="tpu_custom_call", output_to_operand_aliasing={{0}: (6, {}), {1}: (7, {})} | custom-call | flops 335544320 | bytes 67108864 | tf_op jit(solution)/shard_map/cache_write/pallas_call | solution.py:542
  84.0 0.0 collective-permute-done
  84.1 1.3 collective-permute-start.2
  85.4 0.0 collective-permute-done.1
  85.4 83.7 %collective-permute-done.2 = bf16[2,128,2048]{2,1,0:T(8,128)(2,1)S(1)} collective-permute-done((bf16[2,128,2048]{2,1,0:T(8,128)(2,1)}, bf16[2,128,2048]{2,1,0:T(8,128)(2,1)S(1)}, u32[]{:S(2)}, u32[]{:S(2)}) %collective-permute-start.2) | collective-permute-done | bytes 1048608 | tf_op jit(solution)/shard_map/ppermute | solution.py:590
  169.0 2.7 %add_select_fusion = bf16[2,128,2048]{2,1,0:T(8,128)(2,1)} fusion(bf16[2,128,2048]{2,1,0:T(8,128)(2,1)} %get-tuple-element.14, bf16[2,128,2048]{2,1,0:T(8,128)(2,1)S(1)} %collective-permute-done.2, bf16[2,128,2048]{2,1,0:T(8,128)(2,1)} %collective-permute-done, bf16[2,128,2048]{2,1,0:T(8,128)(2,1)} %collective-permute-done.1, pred[]{:T(512)S(6)} %eq.3), kind=kLoop, calls=%fused_computation | loop fusion | flops 1572864 | bytes 5242881 | tf_op jit(solution)/shard_map/jit(_where)/select_n | solution.py:591
Async XLA Ops:
  56.4 27.7 %collective-permute-start = (bf16[2,128,2048]{2,1,0:T(8,128)(2,1)}, bf16[2,128,2048]{2,1,0:T(8,128)(2,1)}, u32[]{:S(2)}, u32[]{:S(2)}) collective-permute-start(bf16[2,128,2048]{2,1,0:T(8,128)(2,1)} %get-tuple-element.14), channel_id=1, source_target_pairs={{3,1},{7,5}} | collective-permute-start | bytes 3145736 | tf_op jit(solution)/shard_map/ppermute | solution.py:587
  58.1 27.3 %collective-permute-start.1 = (bf16[2,128,2048]{2,1,0:T(8,128)(2,1)}, bf16[2,128,2048]{2,1,0:T(8,128)(2,1)}, u32[]{:S(2)}, u32[]{:S(2)}) collective-permute-start(bf16[2,128,2048]{2,1,0:T(8,128)(2,1)} %get-tuple-element.14), channel_id=1, source_target_pairs={{3,2},{7,6}} | collective-permute-start | bytes 3145736 | tf_op jit(solution)/shard_map/ppermute | solution.py:587
  84.1 85.0 %collective-permute-start.2 = (bf16[2,128,2048]{2,1,0:T(8,128)(2,1)}, bf16[2,128,2048]{2,1,0:T(8,128)(2,1)S(1)}, u32[]{:S(2)}, u32[]{:S(2)}) collective-permute-start(bf16[2,128,2048]{2,1,0:T(8,128)(2,1)} %collective-permute-done), channel_id=1, source_target_pairs={{1,0},{5,4}} | collective-permute-start | bytes 3145736 | tf_op jit(solution)/shard_map/ppermute | solution.py:590
where the time goes:
time: 173 us; the launch traced here: 172 us
  waiting for transfers between devices  83.7 us (48%)
  Pallas kernels  80.1 us (46%)
  starting transfers between devices  4.63 us (3%)
  other arithmetic  2.71 us (2%)
    ppermute x1, waiting for transfers between devices, per_device(): from_last.append(lax.ppermute(from_last[0], 'pp', [(1, 0)]))  83.7 us
    pallas_call x1, Pallas kernels, run_layer(): pl.pallas_call(functools.partial(layer_kernel, dims), out_shape=(jax.Shap...  55.1 us
    pallas_call x1, Pallas kernels, write_new(): pl.pallas_call(functools.partial(write_kernel, dims), out_shape=(jax.Shap...  24.3 us
  transfers between devices with their start and end apart: 3, of which 1 were waited for; matrix products, arithmetic and copies ran while one was open for 0% of the time, Pallas kernels for 14%

commit v1 on v0

--- a/solution.py
+++ b/solution.py
@@ -22,7 +22,7 @@
 SLOTS = 8
 NORM_ROWS = 64
 KEEP_SLOTS = 16
-WRITE_SLOTS = 48
+WRITE_SLOTS = 24
 
 
 def rope_freqs(head_dim):
@@ -221,12 +221,9 @@
             probs = (expd / jnp.sum(expd, axis=0, keepdims=True)).astype(BF16).astype(F32)
             sc[...] = jnp.where(hit, 0.0, probs)
             acc = jnp.sum(jnp.where(hit, probs, 0.0), axis=0, keepdims=True) * vnew[g, h].astype(F32)
-            quarter = hd // 4
-            for d in range(4):
-                some = acc[d * quarter:(d + 1) * quarter]
-                for s in range(seq):
-                    some = some + sc[s:s + 1, :] * ring[slot, seq + s, d * quarter:(d + 1) * quarter].astype(F32)
-                qt[pl.ds(pl.multiple_of(h * hd + d * quarter, quarter), quarter), :] = some.astype(BF16)
+            for s in range(seq):
+                acc = acc + sc[s:s + 1, :] * ring[slot, seq + s].astype(F32)
+            qt[rows, :] = acc.astype(BF16)
 
             @pl.when(item + SLOTS < n_kv)
             def _():

time: 173 us -> 172 us (level)
  Pallas kernels: 80.1 us -> 78.2 us
where the time goes in v1:
time: 172 us; the launch traced here: 170 us
  waiting for transfers between devices  83.9 us (49%)
  Pallas kernels  78.2 us (45%)
  starting transfers between devices  4.63 us (3%)
  other arithmetic  2.71 us (2%)
    ppermute x1, waiting for transfers between devices, per_device(): from_last.append(lax.ppermute(from_last[0], 'pp', [(1, 0)]))  83.9 us
    pallas_call x1, Pallas kernels, run_layer(): pl.pallas_call(functools.partial(layer_kernel, dims), out_shape=(jax.Shap...  53.9 us
    pallas_call x1, Pallas kernels, write_new(): pl.pallas_call(functools.partial(write_kernel, dims), out_shape=(jax.Shap...  23.7 us
  transfers between devices with their start and end apart: 3, of which 1 were waited for; matrix products, arithmetic and copies ran while one was open for 0% of the time, Pallas kernels for 14%

profile of v1, /device:TPU:0, one launch (start us, length us, event | category | flops | bytes accessed | tf_op | source)
XLA Modules:
  0.0 170.1 jit_solution(7483086430778411443)
XLA Ops:
  0.6 0.6 cache_keep.1
  1.2 53.9 %layer.1 = (bf16[2,128,2048]{2,1,0:T(8,128)(2,1)}, bf16[2,16,64,128]{3,2,1,0:T(8,128)(2,1)}, bf16[2,16,64,128]{3,2,1,0:T(8,128)(2,1)}) custom-call(s32[65]{0:T(128)} %get-tuple-element.13.after.todo_hbm, s32[2,1,128]{2,1,0:T(1,128)} %bitcast.35, bf16[1,2048]{1,0:T(2,128)(2,1)} %ga_ref.1, bf16[1,2048]{1,0:T(2,128)(2,1)} %gm_ref.1, bf16[2,128,2048]{2,1,0:T(8,128)(2,1)} %hid.1, ...), custom_call_target="tpu_custom_call" | custom-call | tf_op jit(solution)/shard_map/layer/pallas_call | solution.py:346
  55.1 1.7 collective-permute-start
  56.8 1.6 collective-permute-start.1
  58.5 23.7 %cache_write.1 = (bf16[2,16,32,64,128]{4,3,2,1,0:T(8,128)(2,1)}, bf16[2,16,32,64,128]{4,3,2,1,0:T(8,128)(2,1)}) custom-call(s32[65]{0:T(128)} %get-tuple-element.13.after.todo_hbm, s32[2,1,128]{2,1,0:T(1,128)} %bitcast.36, bf16[2,16,64,128]{3,2,1,0:T(8,128)(2,1)} %get-tuple-element.15.knew_hbm, ...), custom_call_target="tpu_custom_call", output_to_operand_aliasing={{0}: (6, {}), {1}: (7, {})} | custom-call | flops 335544320 | bytes 67108864 | tf_op jit(solution)/shard_map/cache_write/pallas_call | solution.py:539
  82.2 0.0 collective-permute-done
  82.2 1.3 collective-permute-start.2
  83.5 0.0 collective-permute-done.1
  83.5 83.9 %collective-permute-done.2 = bf16[2,128,2048]{2,1,0:T(8,128)(2,1)S(1)} collective-permute-done((bf16[2,128,2048]{2,1,0:T(8,128)(2,1)}, bf16[2,128,2048]{2,1,0:T(8,128)(2,1)S(1)}, u32[]{:S(2)}, u32[]{:S(2)}) %collective-permute-start.2) | collective-permute-done | bytes 1048608 | tf_op jit(solution)/shard_map/ppermute | solution.py:587
  167.4 2.7 %add_select_fusion = bf16[2,128,2048]{2,1,0:T(8,128)(2,1)} fusion(bf16[2,128,2048]{2,1,0:T(8,128)(2,1)} %get-tuple-element.14, bf16[2,128,2048]{2,1,0:T(8,128)(2,1)S(1)} %collective-permute-done.2, bf16[2,128,2048]{2,1,0:T(8,128)(2,1)} %collective-permute-done, bf16[2,128,2048]{2,1,0:T(8,128)(2,1)} %collective-permute-done.1, pred[]{:T(512)S(6)} %eq.3), kind=kLoop, calls=%fused_computation | loop fusion | flops 1572864 | bytes 5242881 | tf_op jit(solution)/shard_map/jit(_where)/select_n | solution.py:588
Async XLA Ops:
  55.1 27.0 %collective-permute-start = (bf16[2,128,2048]{2,1,0:T(8,128)(2,1)}, bf16[2,128,2048]{2,1,0:T(8,128)(2,1)}, u32[]{:S(2)}, u32[]{:S(2)}) collective-permute-start(bf16[2,128,2048]{2,1,0:T(8,128)(2,1)} %get-tuple-element.14), channel_id=1, source_target_pairs={{3,1},{7,5}} | collective-permute-start | bytes 3145736 | tf_op jit(solution)/shard_map/ppermute | solution.py:584
  56.8 26.6 %collective-permute-start.1 = (bf16[2,128,2048]{2,1,0:T(8,128)(2,1)}, bf16[2,128,2048]{2,1,0:T(8,128)(2,1)}, u32[]{:S(2)}, u32[]{:S(2)}) collective-permute-start(bf16[2,128,2048]{2,1,0:T(8,128)(2,1)} %get-tuple-element.14), channel_id=1, source_target_pairs={{3,2},{7,6}} | collective-permute-start | bytes 3145736 | tf_op jit(solution)/shard_map/ppermute | solution.py:584
  82.2 85.2 %collective-permute-start.2 = (bf16[2,128,2048]{2,1,0:T(8,128)(2,1)}, bf16[2,128,2048]{2,1,0:T(8,128)(2,1)S(1)}, u32[]{:S(2)}, u32[]{:S(2)}) collective-permute-start(bf16[2,128,2048]{2,1,0:T(8,128)(2,1)} %collective-permute-done), channel_id=1, source_target_pairs={{1,0},{5,4}} | collective-permute-start | bytes 3145736 | tf_op jit(solution)/shard_map/ppermute | solution.py:587

commit v2 on v1

--- a/solution.py
+++ b/solution.py
@@ -259,7 +259,6 @@
             at, col = divmod(c * COLS, hw)
             part = jnp.dot(nbuf[:, 0:hw], wmix[3, at * hw:(at + 1) * hw, col:col + COLS], preferred_element_type=F32)
             hout[g, :, c * COLS:(c + 1) * COLS] = part.astype(BF16)
-        for c in range(n_chunk):
             p_copy(g, c).start()
 
         @pl.when(g == n_groups - 1)

time: 172 us -> 172 us (level); the launches traced: 170 us -> 172 us
  no operation moved by 1% of the time
where the time goes in v2:
time: 172 us
  waiting for transfers between devices  85.3 us (50%)
  Pallas kernels  78.7 us (46%)
  starting transfers between devices  4.63 us (3%)
  other arithmetic  2.71 us (2%)
    ppermute x1, waiting for transfers between devices, per_device(): from_last.append(lax.ppermute(from_last[0], 'pp', [(1, 0)]))  85.3 us
    pallas_call x1, Pallas kernels, run_layer(): pl.pallas_call(functools.partial(layer_kernel, dims), out_shape=(jax.Shap...  54.4 us
    pallas_call x1, Pallas kernels, write_new(): pl.pallas_call(functools.partial(write_kernel, dims), out_shape=(jax.Shap...  23.7 us
  transfers between devices with their start and end apart: 3, of which 1 were waited for; matrix products, arithmetic and copies ran while one was open for 0% of the time, Pallas kernels for 14%

profile of v2, /device:TPU:0, one launch (start us, length us, event | category | flops | bytes accessed | tf_op | source)
XLA Modules:
  0.0 172.0 jit_solution(4504687245369078838)
XLA Ops:
  0.6 0.6 cache_keep.1
  1.2 54.4 %layer.1 = (bf16[2,128,2048]{2,1,0:T(8,128)(2,1)}, bf16[2,16,64,128]{3,2,1,0:T(8,128)(2,1)}, bf16[2,16,64,128]{3,2,1,0:T(8,128)(2,1)}) custom-call(s32[65]{0:T(128)} %get-tuple-element.13.after.todo_hbm, s32[2,1,128]{2,1,0:T(1,128)} %bitcast.35, bf16[1,2048]{1,0:T(2,128)(2,1)} %ga_ref.1, bf16[1,2048]{1,0:T(2,128)(2,1)} %gm_ref.1, bf16[2,128,2048]{2,1,0:T(8,128)(2,1)} %hid.1, ...), custom_call_target="tpu_custom_call" | custom-call | tf_op jit(solution)/shard_map/layer/pallas_call | solution.py:345
  55.7 1.7 collective-permute-start
  57.4 1.6 collective-permute-start.1
  59.0 23.7 %cache_write.1 = (bf16[2,16,32,64,128]{4,3,2,1,0:T(8,128)(2,1)}, bf16[2,16,32,64,128]{4,3,2,1,0:T(8,128)(2,1)}) custom-call(s32[65]{0:T(128)} %get-tuple-element.13.after.todo_hbm, s32[2,1,128]{2,1,0:T(1,128)} %bitcast.36, bf16[2,16,64,128]{3,2,1,0:T(8,128)(2,1)} %get-tuple-element.15.knew_hbm, ...), custom_call_target="tpu_custom_call", output_to_operand_aliasing={{0}: (6, {}), {1}: (7, {})} | custom-call | flops 335544320 | bytes 67108864 | tf_op jit(solution)/shard_map/cache_write/pallas_call | solution.py:538
  82.7 0.0 collective-permute-done
  82.7 1.3 collective-permute-start.2
  84.0 0.0 collective-permute-done.1
  84.0 85.3 %collective-permute-done.2 = bf16[2,128,2048]{2,1,0:T(8,128)(2,1)S(1)} collective-permute-done((bf16[2,128,2048]{2,1,0:T(8,128)(2,1)}, bf16[2,128,2048]{2,1,0:T(8,128)(2,1)S(1)}, u32[]{:S(2)}, u32[]{:S(2)}) %collective-permute-start.2) | collective-permute-done | bytes 1048608 | tf_op jit(solution)/shard_map/ppermute | solution.py:586
  169.3 2.7 %add_select_fusion = bf16[2,128,2048]{2,1,0:T(8,128)(2,1)} fusion(bf16[2,128,2048]{2,1,0:T(8,128)(2,1)} %get-tuple-element.14, bf16[2,128,2048]{2,1,0:T(8,128)(2,1)S(1)} %collective-permute-done.2, bf16[2,128,2048]{2,1,0:T(8,128)(2,1)} %collective-permute-done, bf16[2,128,2048]{2,1,0:T(8,128)(2,1)} %collective-permute-done.1, pred[]{:T(512)S(6)} %eq.3), kind=kLoop, calls=%fused_computation | loop fusion | flops 1572864 | bytes 5242881 | tf_op jit(solution)/shard_map/jit(_where)/select_n | solution.py:587
Async XLA Ops:
  55.7 27.0 %collective-permute-start = (bf16[2,128,2048]{2,1,0:T(8,128)(2,1)}, bf16[2,128,2048]{2,1,0:T(8,128)(2,1)}, u32[]{:S(2)}, u32[]{:S(2)}) collective-permute-start(bf16[2,128,2048]{2,1,0:T(8,128)(2,1)} %get-tuple-element.14), channel_id=1, source_target_pairs={{3,1},{7,5}} | collective-permute-start | bytes 3145736 | tf_op jit(solution)/shard_map/ppermute | solution.py:583
  57.4 26.6 %collective-permute-start.1 = (bf16[2,128,2048]{2,1,0:T(8,128)(2,1)}, bf16[2,128,2048]{2,1,0:T(8,128)(2,1)}, u32[]{:S(2)}, u32[]{:S(2)}) collective-permute-start(bf16[2,128,2048]{2,1,0:T(8,128)(2,1)} %get-tuple-element.14), channel_id=1, source_target_pairs={{3,2},{7,6}} | collective-permute-start | bytes 3145736 | tf_op jit(solution)/shard_map/ppermute | solution.py:583
  82.7 86.6 %collective-permute-start.2 = (bf16[2,128,2048]{2,1,0:T(8,128)(2,1)}, bf16[2,128,2048]{2,1,0:T(8,128)(2,1)S(1)}, u32[]{:S(2)}, u32[]{:S(2)}) collective-permute-start(bf16[2,128,2048]{2,1,0:T(8,128)(2,1)} %collective-permute-done), channel_id=1, source_target_pairs={{1,0},{5,4}} | collective-permute-start | bytes 3145736 | tf_op jit(solution)/shard_map/ppermute | solution.py:586
